TPU v7x, 32 devices: a whole 2x2x4 slice. The times are simulated.
32 devices in a mesh: seq: 8 (over z, x), head: 4 (over y, core).
Axes of the slice: x: 2, y: 2, z: 4, core: 2. Of those that a mesh axis runs over, the one named last changes fastest.
Arguments:
- features: bfloat16 [2048, 1024], P('seq', 'head'), may hold values from -6 to 6
- w_query: bfloat16 [1024, 512], P(None, 'head'), may hold values from -0.1875 to 0.1875
- w_key: bfloat16 [1024, 512], P(None, 'head'), may hold values from -0.1875 to 0.1875
- w_value: bfloat16 [1024, 1024], P(None, 'head'), may hold values from -0.1875 to 0.1875
- w_gate: bfloat16 [1024, 1024], P(None, 'head'), may hold values from -0.1875 to 0.1875
- w_out: bfloat16 [1024, 1024], replicated, may hold values from -0.1875 to 0.1875
- forget: bfloat16 [2, 2048, 512], P(None, 'seq', 'head'), may hold values from -2.5 to 0, as said below
Outputs:
- encoded: bfloat16 [2048, 1024], P('seq', 'head')
Inputs may be any that keep to these rules, and one draw needn't show every extreme that they name: `forget`: every entry is below zero.
All inputs are finite; a program needn't handle non-finite values.
Results may differ from a plain program's by a relative error of at most 0.013.
Values may be sent and summed in bfloat16 or wider, within the bound.
A program may use at most 64 MiB of HBM per device.

v0:
```python
import jax
import jax.numpy as jnp
from jax import lax
from jax.sharding import PartitionSpec as P

HEAD_K = 64
HEAD_V = 128
GROUP = 64


def entering(shard, axis, combine, identity):
    peers, place = (lax.axis_size(axis), lax.axis_index(axis))
    everything = jax.tree.map(lambda part: lax.all_gather(part, axis), shard)
    start = jax.tree.map(
        lambda part, zero: jnp.broadcast_to(jnp.asarray(zero, part.dtype), part.shape),
        shard,
        identity,
    )

    def hop(k, before):
        reached = k < place
        new = combine(before, jax.tree.map(lambda part: part[k], everything))
        return jax.tree.map(lambda a, b: jnp.where(reached, a, b), new, before)

    return lax.fori_loop(0, peers, hop, start)


def entering_2(shard, axis, combine, identity):
    peers, place = (lax.axis_size(axis), lax.axis_index(axis))
    everything = jax.tree.map(
        lambda part, kind: lax.all_gather(part.astype(kind), axis),
        shard,
        (jnp.bfloat16, jnp.bfloat16),
    )
    start = jax.tree.map(
        lambda part, zero: jnp.broadcast_to(jnp.asarray(zero, part.dtype), part.shape),
        shard,
        identity,
    )

    def hop(k, before):
        at = peers - 1 - k
        reached = at > place
        new = combine(
            before, jax.tree.map(lambda part, own: part[at].astype(own.dtype), everything, shard)
        )
        return jax.tree.map(lambda a, b: jnp.where(reached, a, b), new, before)

    return lax.fori_loop(0, peers, hop, start)


def to_blocks(tensor):
    block_count = tensor.shape[0] // GROUP
    return tensor.reshape((block_count, GROUP) + tensor.shape[1:])


def state_increment(memory, key_block, value_block, running):
    finale = running[-1]
    key_to_end = (key_block.astype(jnp.float32) * jnp.exp(finale[None] - running)).astype(
        jnp.bfloat16
    )
    added = jnp.einsum("shi,shj->hij", key_to_end, value_block, preferred_element_type=jnp.float32)
    return jnp.exp(finale)[:, :, None] * memory + added


def block_pass(query_matrix, key_rows, value_rows, decays, initial):
    triangle = jnp.tril(jnp.ones((GROUP, GROUP), jnp.float32))

    def block_advance(memory, blocks):
        query_block, key_block, value_block, decay_block = blocks
        running = jnp.cumsum(decay_block, axis=0)
        query_decayed = (query_block.astype(jnp.float32) * jnp.exp(running)).astype(jnp.bfloat16)
        key_grown = (key_block.astype(jnp.float32) * jnp.exp(-running)).astype(jnp.bfloat16)
        scores = (
            jnp.einsum("thi,shi->hts", query_decayed, key_grown, preferred_element_type=jnp.float32)
            * triangle
        )
        within = jnp.einsum(
            "hts,shj->thj",
            scores.astype(jnp.bfloat16),
            value_block,
            preferred_element_type=jnp.float32,
        )
        carried = jnp.einsum(
            "thi,hij->thj",
            query_decayed.astype(jnp.float32),
            memory,
            precision=lax.Precision.HIGHEST,
        )
        memory = state_increment(memory, key_block, value_block, running)
        return (memory, within + carried)

    blocks = tuple((to_blocks(tensor) for tensor in (query_matrix, key_rows, value_rows, decays)))
    last_memory, outputs = lax.scan(block_advance, initial, blocks)
    return outputs.reshape((query_matrix.shape[0],) + outputs.shape[2:])


def device_summary(key_rows, value_rows, decays):
    heads_here = key_rows.shape[1]

    def device_advance(memory, blocks):
        key_block, value_block, decay_block = blocks
        running = jnp.cumsum(decay_block, axis=0)
        return (state_increment(memory, key_block, value_block, running), None)

    initial = jnp.zeros((heads_here, HEAD_K, HEAD_V), jnp.float32)
    memory, unused = lax.scan(
        device_advance,
        initial,
        tuple((to_blocks(tensor) for tensor in (key_rows, value_rows, decays))),
    )
    total = jnp.sum(decays, axis=0)
    return (total.reshape(-1), memory.reshape(-1, memory.shape[2]))


def combine_states(earlier, latter):
    return (earlier[0] + latter[0], jnp.exp(latter[0])[:, None] * earlier[1] + latter[1])


def local(features, w_query, w_key, w_value, w_gate, w_out, forget):
    row_count = features.shape[0]
    heads_here = w_query.shape[1] // HEAD_K
    columns = lax.all_gather(features, "head", axis=1, tiled=True)
    query_sum, key_sum, value_sum, gating = tuple(
        (
            jnp.dot(columns, weight, preferred_element_type=jnp.float32)
            for weight in (w_query, w_key, w_value, w_gate)
        )
    )
    query_matrix = (query_sum * 0.125).astype(jnp.bfloat16).reshape(row_count, heads_here, HEAD_K)
    key_rows = key_sum.astype(jnp.bfloat16).reshape(row_count, heads_here, HEAD_K)
    value_rows = value_sum.astype(jnp.bfloat16).reshape(row_count, heads_here, HEAD_V)
    decays = forget.astype(jnp.float32).reshape(2, row_count, heads_here, HEAD_K)
    flipped_queries = jnp.flip(query_matrix, 0)
    flipped_keys = jnp.flip(key_rows, 0)
    flipped_values = jnp.flip(value_rows, 0)
    flipped_decays = jnp.flip(decays[1], 0)
    ahead_total, ahead_memory = device_summary(key_rows, value_rows, decays[0])
    behind_total, behind_memory = device_summary(flipped_keys, flipped_values, flipped_decays)
    identity = (jnp.zeros_like(ahead_total), jnp.zeros_like(ahead_memory))
    ahead_inflow = entering((ahead_total, ahead_memory), "seq", combine_states, identity)[1]
    behind_inflow = entering_2((behind_total, behind_memory), "seq", combine_states, identity)[1]
    ahead_out = block_pass(
        query_matrix,
        key_rows,
        value_rows,
        decays[0],
        ahead_inflow.reshape(heads_here, HEAD_K, HEAD_V),
    )
    behind_flipped = block_pass(
        flipped_queries,
        flipped_keys,
        flipped_values,
        flipped_decays,
        behind_inflow.reshape(heads_here, HEAD_K, HEAD_V),
    )
    mixture = ahead_out + jnp.flip(behind_flipped, 0)
    scaled = mixture * lax.rsqrt(jnp.mean(mixture * mixture, axis=-1, keepdims=True) + 1e-06)
    normed = (scaled.reshape(row_count, heads_here * HEAD_V) * jax.nn.silu(gating)).astype(
        jnp.bfloat16
    )
    out_width = w_out.shape[1] // lax.axis_size("head")
    own_columns = lax.dynamic_slice_in_dim(w_out, lax.axis_index("head") * out_width, out_width, 1)
    encoded = jnp.dot(
        lax.all_gather(normed, "head", axis=1, tiled=True),
        own_columns,
        preferred_element_type=jnp.float32,
    )
    return encoded.astype(jnp.bfloat16)


def solution(mesh):
    placed = (
        P("seq", "head"),
        P(None, "head"),
        P(None, "head"),
        P(None, "head"),
        P(None, "head"),
        P(),
        P(None, "seq", "head"),
    )
    return jax.shard_map(
        local, mesh=mesh, in_specs=placed, out_specs=P("seq", "head"), check_vma=False
    )
```

profile of v0, /device:TPU:0, one launch (start us, length us, event | category | flops | bytes accessed | tf_op | source)
XLA Modules:
  0.0 185.7 jit_solution(15773411638401792638)
XLA Ops:
  0.0 1.2 copy.56
  2.2 22.3 %all-gather.2 = bf16[8,1,128]{2,1,0:T(2,128)(2,1)S(1)} all-gather(bf16[1,1,128]{2,1,0:T(2,128)(2,1)S(1)} %reshape.158), channel_id=1, replica_groups=mesh['seq'=8,'head'=4] {'seq'}, dimensions={0}, use_global_device_ids=true | all-gather | bytes 2304 | tf_op jit(solution)/shard_map/all_gather | solution.py:31
  24.6 7.4 %all_gather.21 = bf16[256,1024]{1,0:T(8,128)(2,1)S(1)} all-gather(bf16[256,256]{1,0:T(8,128)(2,1)} %param.19), channel_id=1, replica_groups=mesh['seq'=8,'head'=4] {'head'}, dimensions={1}, use_global_device_ids=true | all-gather | bytes 655360 | tf_op jit(solution)/shard_map/all_gather | solution.py:123
  32.0 1.3 convolution_convert_fusion.2
  34.3 1.4 convolution_convert_fusion.1
  36.4 1.6 rev.21
  38.1 1.5 while.82
  39.6 32.9 %all_gather.24 = bf16[8,128,128]{2,1,0:T(8,128)(2,1)} all-gather(bf16[1,128,128]{2,1,0:T(8,128)(2,1)S(1)} %bitcast.235), channel_id=1, replica_groups=mesh['seq'=8,'head'=4] {'seq'}, dimensions={0}, use_global_device_ids=true | all-gather | bytes 294912 | tf_op jit(solution)/shard_map/all_gather | solution.py:31
  72.5 7.2 %while.83 = (s32[]{:T(128)}, f32[128,128]{1,0:T(8,128)S(1)}, s32[]{:T(128)}, bf16[8,128]{1,0:T(8,128)(2,1)S(1)}, bf16[8,128,128]{2,1,0:T(8,128)(2,1)}, /*index=5*/s32[]{:T(128)}, s32[]{:T(128)}, s32[]{:T(128)}, s32[]{:T(128)}) while((s32[]{:T(128)}, f32[128,128]{1,0:T(8,128)S(1)}, s32[]{:T(128)}, bf16[8,128]{1,0:T(8,128)(2,1)S(1)}, ...), condition=%wide.region_14.15_spmd.clone, body=%wide.region_13.14_spmd.clone.sunk | while | flops 82056 | bytes 165295 | solution.py:49
  72.5 0.9 fusion.173
  73.4 0.9 fusion.173
  74.3 0.9 fusion.173
  75.2 0.9 fusion.173
  76.1 0.9 fusion.173
  77.0 0.9 fusion.173
  77.9 0.9 fusion.173
  78.8 0.9 fusion.173
  79.7 1.3 fusion.78
  82.7 9.1 %while.79 = (s32[]{:T(128)}, f32[2,64,128]{2,1,0:T(8,128)S(1)}, f32[4,64,2,128]{3,1,0,2:T(8,128)}, f32[4,64,2,64]{3,2,1,0:T(2,128)S(1)}, bf16[4,64,2,64]{3,2,1,0...) while((s32[]{:T(128)}, f32[2,64,128]{2,1,0:T(8,128)S(1)}, ...), condition=%wide.region_17.18_spmd.clone, body=%wide.region_15.17_spmd.clone.sunk | while | flops 18497536 | bytes 840297 | solution.py:94
  82.8 0.9 fusion.156
  84.1 0.9 fusion.159
  85.1 0.9 fusion.156
  86.4 0.9 fusion.159
  87.3 0.9 fusion.156
  88.6 0.9 fusion.159
  89.6 0.9 fusion.156
  90.9 0.9 fusion.159
  91.8 1.8 rev.23
  93.7 16.3 %all-gather.1 = f32[8,1,128]{2,1,0:T(1,128)S(1)} all-gather(f32[1,1,128]{2,1,0:T(1,128)S(1)} %bitcast.237), channel_id=2, replica_groups=mesh['seq'=8,'head'=4] {'seq'}, dimensions={0}, use_global_device_ids=true | all-gather | bytes 4608 | tf_op jit(solution)/shard_map/all_gather | solution.py:13
  110.0 1.7 reshape_squeeze.4
  111.7 1.1 copy.58
  112.8 1.0 reshape_reshape.11
  114.6 0.9 reshape.169
  115.5 1.1 copy.60
  116.6 4.6 %while.80 = (s32[]{:T(128)}, f32[2,64,128]{2,1,0:T(8,128)S(1)}, f32[4,64,2,64]{3,2,1,0:T(2,128)S(1)}, bf16[4,64,2,64]{3,2,1,0:T(2,128)(2,1)}, bf16[4,64,2,128]{3,1,2,0:T(8,128)(2,1)S(1)}, /*index=5*/s32[]{:T(128)}, s32[]{:T(128)}) while((s32[]{:T(128)}, f32[2,64,128]{2,1,0:T(8,128)S(1)}, f32[4,64,2,64]{3,2,1,0:T(2,128)S(1)}, ...), condition=%wide.region_3.4_spmd.clone, body=%wide.region_1.3_spmd.clone.sunk | while | flops 2695171 | bytes 364139 | solution.py:107
  116.7 0.8 fusion.164
  117.8 0.8 fusion.164
  119.0 0.8 fusion.164
  120.1 0.8 fusion.164
  121.2 33.3 %all_gather.22 = f32[8,128,128]{2,1,0:T(8,128)} all-gather(f32[1,128,128]{2,1,0:T(8,128)S(1)} %bitcast.227), channel_id=1, replica_groups=mesh['seq'=8,'head'=4] {'seq'}, dimensions={0}, use_global_device_ids=true | all-gather | bytes 589824 | tf_op jit(solution)/shard_map/all_gather | solution.py:13
  154.5 7.8 %while.81 = (s32[]{:T(128)}, f32[128,128]{1,0:T(8,128)S(1)}, s32[]{:T(128)}, f32[8,128]{1,0:T(8,128)S(1)}, f32[8,128,128]{2,1,0:T(8,128)}, /*index=5*/s32[]{:T(128)}, s32[]{:T(128)}) while((s32[]{:T(128)}, f32[128,128]{1,0:T(8,128)S(1)}, s32[]{:T(128)}, f32[8,128]{1,0:T(8,128)S(1)}, f32[8,128,128]{2,1,0:T(8,128)}, ...), condition=%wide.region_5.6_spmd.clone, body=%wide.region_4.5_spmd.clone.sunk | while | flops 65540 | bytes 198257 | solution.py:25
  154.5 0.9 fusion.166
  155.5 0.9 fusion.166
  156.4 0.9 fusion.166
  157.4 0.9 fusion.166
  158.4 0.9 fusion.166
  159.4 0.9 fusion.166
  160.4 0.9 fusion.166
  161.3 0.9 fusion.166
  163.1 1.7 copy.64
  165.5 9.2 %while.78 = (s32[]{:T(128)}, f32[2,64,128]{2,1,0:T(8,128)S(1)}, f32[4,64,2,128]{3,1,0,2:T(8,128)}, f32[4,64,2,64]{3,2,1,0:T(2,128)S(1)}, bf16[4,64,2,64]{3,2,1,0...) while((s32[]{:T(128)}, f32[2,64,128]{2,1,0:T(8,128)S(1)}, ...), condition=%wide.region_8.9_spmd.clone, body=%wide.region_6.8_spmd.clone.sunk | while | flops 18497536 | bytes 840297 | solution.py:94
  165.6 0.9 fusion.143
  166.9 0.9 fusion.146
  167.9 0.9 fusion.143
  169.2 0.9 fusion.146
  170.2 0.9 fusion.143
  171.5 0.9 fusion.146
  172.4 0.9 fusion.143
  173.8 0.9 fusion.146
  174.7 1.1 multiply_reduce_fusion
  175.8 1.1 multiply_bitcast_fusion
  176.9 1.4 fusion.80
  178.2 6.5 %all_gather.25 = bf16[256,1024]{1,0:T(8,128)(2,1)S(1)} all-gather(bf16[256,256]{1,0:T(8,128)(2,1)S(1)} %fusion.80), channel_id=1, replica_groups=mesh['seq'=8,'head'=4] {'head'}, dimensions={1}, use_global_device_ids=true | all-gather | bytes 655360 | tf_op jit(solution)/shard_map/all_gather | solution.py:165
  184.7 1.0 convolution_convert_fusion
  (136 shorter events, 13.3 us)
Async XLA Ops:
  0.0 184.7 %copy-start = (bf16[1024,1024]{1,0:T(8,128)(2,1)S(1)}, bf16[1024,1024]{1,0:T(8,128)(2,1)}, u32[]{:S(2)}) copy-start(bf16[1024,1024]{1,0:T(8,128)(2,1)} %param.24) | copy-start | bytes 6291460
  33.3 0.6 copy-start.3
  35.7 2.4 %copy-start.1 = (bf16[256,256]{0,1:T(8,128)(2,1)}, bf16[256,256]{0,1:T(8,128)(2,1)S(1)}, u32[]{:S(2)}) copy-start(bf16[256,256]{0,1:T(8,128)(2,1)S(1)} %convolution_convert_fusion.1) | copy-start | bytes 393220
  81.0 1.7 copy-start.4
  91.8 22.8 %copy-start.2 = (bf16[256,256]{0,1:T(8,128)(2,1)S(1)}, bf16[256,256]{0,1:T(8,128)(2,1)}, u32[]{:S(2)}) copy-start(bf16[256,256]{0,1:T(8,128)(2,1)} %copy-done.1) | copy-start | bytes 393220
  116.6 45.7 %copy-start.5 = (bf16[256,128]{0,1:T(8,128)(2,1)S(1)}, bf16[256,128]{0,1:T(8,128)(2,1)}, u32[]{:S(2)}) copy-start(bf16[256,128]{0,1:T(8,128)(2,1)} %copy-done.4) | copy-start | bytes 196612
where the time goes:
time: 188 us; the launch traced here: 186 us
  blocking collectives  119 us (63%)
  other arithmetic  28.8 us (15%)
  local copies, waits for them, and re-layouts  19 us (10%)
  matrix products  17.9 us (10%)
    all_gather x2, blocking collectives, entering_2(): lax.all_gather(part.astype(kind), axis)  55.1 us
    all_gather x2, blocking collectives, entering(): everything = jax.tree.map(lambda part: lax.all_gather(part, axis), shard)  49.6 us
    select_n x16, other arithmetic, hop(): return jax.tree.map(lambda a, b: jnp.where(reached, a, b), new, before)  14.3 us
    all_gather x1, blocking collectives, local(): columns = lax.all_gather(features, 'head', axis=1, tiled=True)  7.41 us
    convert_element_type x8, other arithmetic, block_advance(): (key_block.astype(jnp.float32) * jnp.exp(-running)).astype(jnp.bfloat16)  7.24 us
    dot_general x8, matrix products, block_advance(): jnp.einsum('hts,shj->thj', scores.astype(jnp.bfloat16), value_block, pref...  7.07 us
    unnamed x21, local copies, waits for them, and re-layouts  6.77 us
    all_gather x1, blocking collectives, local(): lax.all_gather(normed, 'head', axis=1, tiled=True)  6.51 us

commit v1 on v0

v1 whole, which is shorter than its diff:
```python
import functools

import jax
import jax.numpy as jnp
from jax import lax
from jax.experimental import pallas as pl
from jax.experimental.pallas import tpu as pltpu
from jax.sharding import PartitionSpec as P

HEAD_K = 64
HEAD_V = 128
GROUP = 64
CHUNKS = 2
MESH = pl.DeviceIdType.MESH
F32 = jnp.float32
BF16 = jnp.bfloat16
NT = (((1,), (1,)), ((), ()))
TN = (((0,), (0,)), ((), ()))


def dot(a, b):
    return jnp.dot(a, b, preferred_element_type=F32)


def each(count, start, body):
    if count - start <= 16:
        for i in range(start, count):
            body(i)
    else:
        lax.fori_loop(start, count, lambda i, c: (body(i), c)[1], 0)


class HeadGather:
    def __init__(self, heads, me, own, slots, rows, cs, cr, ss, sr):
        self.chips = heads // 2
        self.core = lax.rem(me, 2)
        self.chip = lax.div(me, 2)
        self.me, self.own, self.slots, self.rows = me, own, slots, rows
        self.sib = me + 1 - 2 * self.core
        self.cs, self.cr, self.ss, self.sr = cs, cr, ss, sr
        self.started = []

    def cut(self, ref, c):
        return ref.at[pl.ds(c * self.rows, self.rows), :]

    def cross_origin(self, j):
        return lax.rem(self.chip - j + self.chips, self.chips) * 2 + self.core

    def handed_origin(self, j):
        return lax.rem(self.chip - j + self.chips, self.chips) * 2 + 1 - self.core

    def cross(self, j, c):
        target = lax.rem(self.chip + j, self.chips) * 2 + self.core
        return pltpu.make_async_remote_copy(
            src_ref=self.cut(self.own, c),
            dst_ref=self.cut(self.slots.at[self.me], c),
            send_sem=self.cs.at[j, c],
            recv_sem=self.cr.at[j, c],
            device_id={"head": target},
            device_id_type=MESH,
        )

    def side(self, j, c):
        origin = self.me if j == 0 else self.cross_origin(j)
        src = self.own if j == 0 else self.slots.at[origin]
        return pltpu.make_async_remote_copy(
            src_ref=self.cut(src, c),
            dst_ref=self.cut(self.slots.at[origin], c),
            send_sem=self.ss.at[j, c],
            recv_sem=self.sr.at[j, c],
            device_id={"head": self.sib},
            device_id_type=MESH,
        )

    def start(self, c):
        for j in range(1, self.chips):
            copy = self.cross(j, c)
            copy.start()
            self.started.append(copy)
        copy = self.side(0, c)
        copy.start()
        self.started.append(copy)

    def hand_on(self, j, c):
        self.cross(j, c).wait_recv()
        copy = self.side(j, c)
        copy.start()
        self.started.append(copy)

    def finish(self):
        for copy in self.started:
            copy.wait_send()


def kernel(
    heads, seqs,
    feat_hbm, wq_hbm, wk_hbm, wv_hbm, wg_hbm, wo_hbm, forget_hbm,
    out_ref,
    feat, w_s, wo_s, fg, acc, mults, edge, tots, wts, st, recv, vals, keys, ps, mix, nrm,
    own_sem, w_sem, wo_sem, fg_sem,
    fcs, fcr, fss, fsr, ncs, ncr, nss, nsr, ts, tr, xs, xr,
):
    h = lax.axis_index("head")
    p = lax.axis_index("seq")
    rows, width = feat_hbm.shape
    kw = wq_hbm.shape[1]
    vw = wv_hbm.shape[1]
    blocks = rows // GROUP
    crows = rows // CHUNKS
    k0, v0, q0, g0 = 0, kw, kw + vw, kw + vw + kw

    fg_copy = pltpu.make_async_copy(forget_hbm, fg, fg_sem)
    fg_copy.start()
    own_copy = pltpu.make_async_copy(feat_hbm, feat.at[h], own_sem)
    own_copy.start()
    w_copies = []
    for i in range(heads):
        for n, (src, at, wide) in enumerate(
            ((wk_hbm, k0, kw), (wv_hbm, v0, vw), (wq_hbm, q0, kw), (wg_hbm, g0, vw))
        ):
            copy = pltpu.make_async_copy(
                src.at[pl.ds(i * width, width), :],
                w_s.at[i, :, pl.ds(at, wide)],
                w_sem.at[i, n],
            )
            copy.start()
            w_copies.append(copy)
    wo_copies = []
    ow = out_ref.shape[1]
    for i in range(heads):
        copy = pltpu.make_async_copy(
            wo_hbm.at[pl.ds(i * vw, vw), pl.ds(pl.multiple_of(h * ow, ow), ow)],
            wo_s.at[i],
            wo_sem.at[i],
        )
        copy.start()
        wo_copies.append(copy)

    barrier = pltpu.get_barrier_semaphore()
    for j in range(1, heads):
        pl.semaphore_signal(
            barrier, inc=1, device_id={"head": lax.rem(h + j, heads)}, device_id_type=MESH
        )
    each(
        seqs,
        1,
        lambda d: pl.semaphore_signal(
            barrier, inc=1, device_id={"seq": lax.rem(p + d, seqs)}, device_id_type=MESH
        ),
    )
    pl.semaphore_wait(barrier, heads - 1 + seqs - 1)

    gather = HeadGather(heads, h, feat_hbm, feat, crows, fcs, fcr, fss, fsr)
    for c in range(CHUNKS):
        gather.start(c)

    fg_copy.wait()
    tok = lax.broadcasted_iota(jnp.int32, (rows, rows), 0)
    src = lax.broadcasted_iota(jnp.int32, (rows, rows), 1)
    same = (tok // GROUP) == (src // GROUP)
    row = lax.broadcasted_iota(jnp.int32, (rows, kw), 0)
    lane = lax.broadcasted_iota(jnp.int32, (rows, kw), 1)
    edge[...] = jnp.zeros_like(edge)
    whole_sums, block_sums = [], []
    for d in range(2):
        order = (src <= tok) if d == 0 else (src >= tok)
        f = fg[d]
        whole = dot(jnp.where(order, 1.0, 0.0).astype(BF16), f)
        block = dot(jnp.where(order & same, 1.0, 0.0).astype(BF16), f)
        total = whole[rows - 1 : rows] if d == 0 else whole[0:1]
        edge[d : d + 1, :] = total
        whole_sums.append(whole)
        block_sums.append(block)

    def total_copy(d):
        return pltpu.make_async_remote_copy(
            src_ref=edge,
            dst_ref=tots.at[p],
            send_sem=ts.at[d],
            recv_sem=tr.at[d],
            device_id={"seq": lax.rem(p + d, seqs)},
            device_id_type=MESH,
        )

    for d in range(2):
        whole, block = whole_sums[d], block_sums[d]
        total = whole[rows - 1 : rows] if d == 0 else whole[0:1]
        mults[d, blocks] = jnp.exp(block)
        mults[d, blocks + 1] = jnp.exp(total - whole)
        mults[d, blocks + 2] = jnp.exp(whole)
        for i in range(blocks):
            lo, hi = i * GROUP, (i + 1) * GROUP
            inside = (row >= lo) & (row < hi)
            if d == 0:
                past = row < lo
                start = whole[lo - 1 : lo] if i else jnp.zeros((1, kw), F32)
            else:
                past = row >= hi
                start = whole[hi : hi + 1] if i < blocks - 1 else jnp.zeros((1, kw), F32)
            power = jnp.where(past, start - whole, jnp.where(inside, -block, -jnp.inf))
            mults[d, i] = jnp.exp(power)
    each(seqs, 1, lambda d: total_copy(d).start())

    own_copy.wait()
    for copy in w_copies:
        copy.wait()
    acc[...] = dot(feat[h], w_s[h])
    gather.hand_on(1, 0)
    for c in range(CHUNKS):
        gather.side(0, c).wait_recv()
    acc[...] += dot(feat[gather.sib], w_s[gather.sib])
    for j in range(1, gather.chips):
        for c in range(CHUNKS):
            if j > 1 or c > 0:
                gather.hand_on(j, c)
        at = gather.cross_origin(j)
        if j < gather.chips - 1:
            acc[...] += dot(feat[at], w_s[at])
        else:
            acc[...] += dot(feat[at], w_s[at])
        for c in range(CHUNKS):
            gather.side(j, c).wait_recv()
        at = gather.handed_origin(j)
        if j < gather.chips - 1:
            acc[...] += dot(feat[at], w_s[at])
    last = gather.handed_origin(gather.chips - 1)
    kv = acc[:, :q0] + dot(feat[last], w_s[last, :, :q0])
    key = kv[:, :kw].astype(BF16)
    val = kv[:, kw:].astype(BF16)
    keys[...] = key
    vals[...] = val

    keyf = key.astype(F32)
    grown = jnp.concatenate(
        [(keyf * mults[d, blocks + 1]).astype(BF16) for d in range(2)], axis=1
    )
    state = lax.dot_general(val, grown, TN, preferred_element_type=F32)
    slane = lax.broadcasted_iota(jnp.int32, (HEAD_V, kw), 1)
    heads_here = kw // HEAD_K
    for d in range(2):
        packed = state[:HEAD_V, d * kw : (d + 1) * kw]
        for g in range(1, heads_here):
            packed = jnp.where(
                slane >= g * HEAD_K,
                state[g * HEAD_V : (g + 1) * HEAD_V, d * kw : (d + 1) * kw],
                packed,
            )
        st[d] = packed.astype(BF16)

    def state_copy(d):
        q = lax.rem(p + d, seqs)
        return pltpu.make_async_remote_copy(
            src_ref=st.at[jnp.where(q > p, 0, 1)],
            dst_ref=recv.at[p],
            send_sem=xs.at[d],
            recv_sem=xr.at[d],
            device_id={"seq": q},
            device_id_type=MESH,
        )

    each(seqs, 1, lambda d: state_copy(d).start())

    qg = acc[:, q0:] + dot(feat[last], w_s[last, :, q0:])
    query = (qg[:, :kw] * 0.125).astype(BF16).astype(F32)
    gate = qg[:, kw:]
    acc[:, :vw] = gate / (1.0 + jnp.exp(-gate))
    qd = [(query * mults[d, blocks]).astype(BF16) for d in range(2)]
    qdev = jnp.concatenate(
        [(query * mults[d, blocks + 2]).astype(BF16) for d in range(2)], axis=1
    )
    blane = lax.broadcasted_iota(jnp.int32, (GROUP, kw), 1) // HEAD_K
    bt = lax.rem(lax.broadcasted_iota(jnp.int32, (heads_here * GROUP, rows), 0), GROUP)
    bs = lax.broadcasted_iota(jnp.int32, (heads_here * GROUP, rows), 1)
    for i in range(blocks):
        scores = []
        for d in range(2):
            qb = qd[d][i * GROUP : (i + 1) * GROUP]
            stacked = jnp.concatenate(
                [jnp.where(blane == g, qb, jnp.zeros_like(qb)) for g in range(heads_here)], axis=0
            )
            grown_keys = (keyf * mults[d, i]).astype(BF16)
            part = lax.dot_general(stacked, grown_keys, NT, preferred_element_type=F32)
            keep = (bs <= bt + i * GROUP) if d == 0 else (bs >= bt + i * GROUP)
            scores.append(jnp.where(keep, part, 0.0))
        both = (scores[0] + scores[1]).astype(BF16)
        for g in range(heads_here):
            ps[g, i * GROUP : (i + 1) * GROUP, :] = both[g * GROUP : (g + 1) * GROUP]
    for g in range(heads_here):
        cols = slice(g * HEAD_V, (g + 1) * HEAD_V)
        mix[:, cols] = dot(ps[g], val[:, cols])

    each(seqs, 1, lambda d: total_copy(d).wait_recv())
    tots[p] = jnp.zeros_like(edge)

    def weigh(j, sums):
        ahead, behind = sums
        k = p - j
        ok = k >= 0
        at = jnp.maximum(k, 0)
        wts[j, 0:1, :] = jnp.where(ok, jnp.exp(ahead), 0.0)
        ahead = ahead + jnp.where(ok, tots[at, 0:1, :], 0.0)
        k = p + j
        ok = k < seqs
        at = jnp.minimum(k, seqs - 1)
        wts[seqs - j, 1:2, :] = jnp.where(ok, jnp.exp(behind), 0.0)
        behind = behind + jnp.where(ok, tots[at, 1:2, :], 0.0)
        return ahead, behind

    zero = jnp.zeros((1, kw), F32)
    sums = (zero, zero)
    if seqs <= 16:
        for j in range(1, seqs):
            sums = weigh(j, sums)
    else:
        lax.fori_loop(1, seqs, weigh, sums)

    def gain(d, inflow):
        state_copy(d).wait_recv()
        part = recv[lax.rem(p - d + seqs, seqs)].astype(F32)
        return inflow[0] + part * wts[d, 0:1, :], inflow[1] + part * wts[d, 1:2, :]

    none = jnp.zeros((HEAD_V, kw), F32)
    inflow = (none, none)
    if seqs <= 16:
        for d in range(1, seqs):
            inflow = gain(d, inflow)
    else:
        inflow = lax.fori_loop(1, seqs, gain, inflow)
    spread = jnp.concatenate(
        [
            jnp.concatenate(
                [jnp.where(slane // HEAD_K == g, inflow[d], 0.0) for g in range(heads_here)], axis=0
            )
            for d in range(2)
        ],
        axis=1,
    ).astype(BF16)

    tail = HeadGather(heads, h, nrm.at[h], nrm, crows, ncs, ncr, nss, nsr)
    for c in range(CHUNKS):
        at = slice(c * crows, (c + 1) * crows)
        whole = mix[at, :] + lax.dot_general(qdev[at], spread, NT, preferred_element_type=F32)
        for g in range(heads_here):
            cols = slice(g * HEAD_V, (g + 1) * HEAD_V)
            part = whole[:, cols]
            scale = lax.rsqrt(jnp.mean(part * part, axis=-1, keepdims=True) + 1e-06)
            nrm[h, at, cols] = (part * scale * acc[at, cols]).astype(BF16)
        tail.start(c)

    for copy in wo_copies:
        copy.wait()
    for c in range(CHUNKS):
        at = slice(c * crows, (c + 1) * crows)
        total = dot(nrm[h, at, :], wo_s[h])
        tail.side(0, c).wait_recv()
        total += dot(nrm[tail.sib, at, :], wo_s[tail.sib])
        for j in range(1, tail.chips):
            tail.hand_on(j, c)
            origin = tail.cross_origin(j)
            total += dot(nrm[origin, at, :], wo_s[origin])
            tail.side(j, c).wait_recv()
            origin = tail.handed_origin(j)
            total += dot(nrm[origin, at, :], wo_s[origin])
        out_ref[at, :] = total.astype(BF16)

    gather.finish()
    tail.finish()
    each(seqs, 1, lambda d: total_copy(d).wait_send())
    each(seqs, 1, lambda d: state_copy(d).wait_send())


def solution(mesh):
    heads, seqs = mesh.shape["head"], mesh.shape["seq"]

    def local(features, w_query, w_key, w_value, w_gate, w_out, forget):
        rows, width = features.shape
        kw, vw = w_query.shape[1], w_value.shape[1]
        ow = w_out.shape[1] // heads
        blocks = rows // GROUP
        chips = heads // 2
        dma = pltpu.SemaphoreType.DMA
        hop = dma((chips, CHUNKS))
        return pl.pallas_call(
            functools.partial(kernel, heads, seqs),
            out_shape=jax.ShapeDtypeStruct((rows, ow), BF16),
            in_specs=[pl.BlockSpec(memory_space=pl.ANY)] * 7,
            out_specs=pl.BlockSpec(memory_space=pltpu.VMEM),
            scratch_shapes=[
                pltpu.VMEM((heads, rows, width), BF16),
                pltpu.VMEM((heads, width, 2 * (kw + vw)), BF16),
                pltpu.VMEM((heads, vw, ow), BF16),
                pltpu.VMEM((2, rows, kw), BF16),
                pltpu.VMEM((rows, 2 * (kw + vw)), F32),
                pltpu.VMEM((2, blocks + 3, rows, kw), F32),
                pltpu.VMEM((8, kw), F32),
                pltpu.VMEM((seqs, 8, kw), F32),
                pltpu.VMEM((seqs, 8, kw), F32),
                pltpu.VMEM((2, HEAD_V, kw), BF16),
                pltpu.VMEM((seqs, HEAD_V, kw), BF16),
                pltpu.VMEM((rows, vw), BF16),
                pltpu.VMEM((rows, kw), BF16),
                pltpu.VMEM((kw // HEAD_K, rows, rows), BF16),
                pltpu.VMEM((rows, vw), F32),
                pltpu.VMEM((heads, rows, vw), BF16),
                dma,
                dma((heads, 4)),
                dma((heads,)),
                dma,
                hop, hop, hop, hop, hop, hop, hop, hop,
                dma((seqs,)), dma((seqs,)), dma((seqs,)), dma((seqs,)),
            ],
            compiler_params=pltpu.CompilerParams(
                collective_id=0, has_side_effects=True, vmem_limit_bytes=40 * 1024 * 1024
            ),
        )(features, w_query, w_key, w_value, w_gate, w_out, forget)

    placed = (
        P("seq", "head"),
        P(None, "head"),
        P(None, "head"),
        P(None, "head"),
        P(None, "head"),
        P(),
        P(None, "seq", "head"),
    )
    return jax.shard_map(
        local, mesh=mesh, in_specs=placed, out_specs=P("seq", "head"), check_vma=False
    )
```

time: 188 us -> 32.9 us (0.17)
  the two profiles are of different devices: /device:TPU:0 before, /device:TPU:15 now
where the time goes in v1:
time: 32.9 us; the launch traced here: 32.5 us
  Pallas kernels  24.5 us (74%)
  local copies, waits for them, and re-layouts  8.04 us (24%)
    pallas_call x1, Pallas kernels, local(): pl.pallas_call(functools.partial(kernel, heads, seqs), out_shape=jax.Shap...  24.5 us
    unnamed x15, local copies, waits for them, and re-layouts  8.04 us

profile of v1, /device:TPU:15, one launch (start us, length us, event | category | flops | bytes accessed | tf_op | source)
XLA Modules:
  0.0 32.5 jit_solution(3496279682285183859)
XLA Ops:
  0.0 0.0 copy-start
  0.0 1.6 %copy-done = bf16[1024,1024]{1,0:T(8,128)(2,1)S(1)} copy-done((bf16[1024,1024]{1,0:T(8,128)(2,1)S(1)}, bf16[1024,1024]{1,0:T(8,128)(2,1)}, u32[]{:S(2)}) %copy-start) | copy-done | bytes 2097176
  1.6 0.0 copy-start.1
  1.6 1.0 %copy-done.1 = bf16[1024,256]{1,0:T(8,128)(2,1)S(1)} copy-done((bf16[1024,256]{1,0:T(8,128)(2,1)S(1)}, bf16[1024,256]{1,0:T(8,128)(2,1)}, u32[]{:S(2)}) %copy-start.1) | copy-done | bytes 524312
  2.6 0.0 copy-start.2
  2.6 1.0 %copy-done.2 = bf16[1024,256]{1,0:T(8,128)(2,1)S(1)} copy-done((bf16[1024,256]{1,0:T(8,128)(2,1)S(1)}, bf16[1024,256]{1,0:T(8,128)(2,1)}, u32[]{:S(2)}) %copy-start.2) | copy-done | bytes 524312
  3.7 0.0 copy-start.3
  3.7 0.9 %copy-done.3 = bf16[1024,128]{1,0:T(8,128)(2,1)S(1)} copy-done((bf16[1024,128]{1,0:T(8,128)(2,1)S(1)}, bf16[1024,128]{1,0:T(8,128)(2,1)}, u32[]{:S(2)}) %copy-start.3) | copy-done | bytes 262168
  4.6 0.0 copy-start.4
  4.6 0.9 %copy-done.4 = bf16[1024,128]{1,0:T(8,128)(2,1)S(1)} copy-done((bf16[1024,128]{1,0:T(8,128)(2,1)S(1)}, bf16[1024,128]{1,0:T(8,128)(2,1)}, u32[]{:S(2)}) %copy-start.4) | copy-done | bytes 262168
  5.6 0.0 copy-start.5
  5.6 0.9 %copy-done.5 = bf16[256,256]{1,0:T(8,128)(2,1)S(1)} copy-done((bf16[256,256]{1,0:T(8,128)(2,1)S(1)}, bf16[256,256]{1,0:T(8,128)(2,1)}, u32[]{:S(2)}) %copy-start.5) | copy-done | bytes 131096
  6.5 0.0 copy-start.6
  6.5 0.9 %copy-done.6 = bf16[2,256,128]{2,1,0:T(8,128)(2,1)S(1)} copy-done((bf16[2,256,128]{2,1,0:T(8,128)(2,1)S(1)}, bf16[2,256,128]{2,1,0:T(8,128)(2,1)}, u32[]{:S(2)}) %copy-start.6) | copy-done | bytes 131096
  7.4 24.5 %shard_map.73 = bf16[256,256]{1,0:T(8,128)(2,1)S(1)} custom-call(bf16[256,256]{1,0:T(8,128)(2,1)S(1)} %copy-done.5, bf16[1024,128]{1,0:T(8,128)(2,1)S(1)} %copy-done.3, bf16[1024,128]{1,0:T(8,128)(2,1)S(1)} %copy-done.4, bf16[1024,256]{1,0:T(8,128)(2,1)S(1)} %copy-done.1, bf16[1024,256]{1,0:T(8,128)(2,1)S(1)} %copy-done.2, bf16[1024,1024]{1,0:T(8,128)(2,1)S(1)} %copy-done, ...), custom_call_target="tpu_custom_call" | custom-call | tf_op jit(solution)/shard_map/pallas_call | solution.py:383
  31.9 0.7 %copy.9 = bf16[256,256]{1,0:T(8,128)(2,1)} copy(bf16[256,256]{1,0:T(8,128)(2,1)S(1)} %shard_map.73) | data formatting | bytes 262144
Async XLA Ops:
  0.0 1.6 %copy-start = (bf16[1024,1024]{1,0:T(8,128)(2,1)S(1)}, bf16[1024,1024]{1,0:T(8,128)(2,1)}, u32[]{:S(2)}) copy-start(bf16[1024,1024]{1,0:T(8,128)(2,1)} %wo_hbm.1) | copy-start | bytes 6291460
  1.6 1.0 %copy-start.1 = (bf16[1024,256]{1,0:T(8,128)(2,1)S(1)}, bf16[1024,256]{1,0:T(8,128)(2,1)}, u32[]{:S(2)}) copy-start(bf16[1024,256]{1,0:T(8,128)(2,1)} %wv_hbm.1) | copy-start | bytes 1572868
  2.6 1.0 %copy-start.2 = (bf16[1024,256]{1,0:T(8,128)(2,1)S(1)}, bf16[1024,256]{1,0:T(8,128)(2,1)}, u32[]{:S(2)}) copy-start(bf16[1024,256]{1,0:T(8,128)(2,1)} %wg_hbm.1) | copy-start | bytes 1572868
  3.7 0.9 %copy-start.3 = (bf16[1024,128]{1,0:T(8,128)(2,1)S(1)}, bf16[1024,128]{1,0:T(8,128)(2,1)}, u32[]{:S(2)}) copy-start(bf16[1024,128]{1,0:T(8,128)(2,1)} %wq_hbm.1) | copy-start | bytes 786436
  4.6 0.9 %copy-start.4 = (bf16[1024,128]{1,0:T(8,128)(2,1)S(1)}, bf16[1024,128]{1,0:T(8,128)(2,1)}, u32[]{:S(2)}) copy-start(bf16[1024,128]{1,0:T(8,128)(2,1)} %wk_hbm.1) | copy-start | bytes 786436
  5.6 0.9 %copy-start.5 = (bf16[256,256]{1,0:T(8,128)(2,1)S(1)}, bf16[256,256]{1,0:T(8,128)(2,1)}, u32[]{:S(2)}) copy-start(bf16[256,256]{1,0:T(8,128)(2,1)} %feat_hbm.1) | copy-start | bytes 393220
  6.5 0.9 %copy-start.6 = (bf16[2,256,128]{2,1,0:T(8,128)(2,1)S(1)}, bf16[2,256,128]{2,1,0:T(8,128)(2,1)}, u32[]{:S(2)}) copy-start(bf16[2,256,128]{2,1,0:T(8,128)(2,1)} %forget_hbm.1) | copy-start | bytes 393220

commit v2 on v1

--- a/solution.py
+++ b/solution.py
@@ -98,7 +98,7 @@
     out_ref,
     feat, w_s, wo_s, fg, acc, mults, edge, tots, wts, st, recv, vals, keys, ps, mix, nrm,
     own_sem, w_sem, wo_sem, fg_sem,
-    fcs, fcr, fss, fsr, ncs, ncr, nss, nsr, ts, tr, xs, xr,
+    fcs, fcr, fss, fsr, ncs, ncr, nss, nsr, ts, tr, xs, xr, meet,
 ):
     h = lax.axis_index("head")
     p = lax.axis_index("seq")
@@ -136,19 +136,35 @@
         copy.start()
         wo_copies.append(copy)
 
+    def near(sem, d):
+        @pl.when(p >= d)
+        def _():
+            pl.semaphore_signal(sem, inc=1, device_id={"seq": p - d}, device_id_type=MESH)
+
+        @pl.when(p + d < seqs)
+        def _():
+            pl.semaphore_signal(sem, inc=1, device_id={"seq": p + d}, device_id_type=MESH)
+
+    def near_count(d):
+        return jnp.where(p >= d, 1, 0) + jnp.where(p + d < seqs, 1, 0)
+
     barrier = pltpu.get_barrier_semaphore()
-    for j in range(1, heads):
+    sibling = h + 1 - 2 * lax.rem(h, 2)
+    pl.semaphore_signal(barrier, inc=1, device_id={"head": sibling}, device_id_type=MESH)
+    for j in range(2, heads, 2):
         pl.semaphore_signal(
             barrier, inc=1, device_id={"head": lax.rem(h + j, heads)}, device_id_type=MESH
         )
-    each(
-        seqs,
-        1,
-        lambda d: pl.semaphore_signal(
-            barrier, inc=1, device_id={"seq": lax.rem(p + d, seqs)}, device_id_type=MESH
-        ),
-    )
-    pl.semaphore_wait(barrier, heads - 1 + seqs - 1)
+    near(barrier, 1)
+    pl.semaphore_wait(barrier, heads // 2 + near_count(1))
+
+    rounds = meet.shape[0]
+    near(meet.at[0], 1)
+
+    def met(r):
+        pl.semaphore_wait(meet.at[r], near_count(1 << r))
+        if r + 1 < rounds:
+            near(meet.at[r + 1], 1 << (r + 1))
 
     gather = HeadGather(heads, h, feat_hbm, feat, crows, fcs, fcr, fss, fsr)
     for c in range(CHUNKS):
@@ -172,6 +188,8 @@
         whole_sums.append(whole)
         block_sums.append(block)
 
+    met(0)
+
     def total_copy(d):
         return pltpu.make_async_remote_copy(
             src_ref=edge,
@@ -199,13 +217,17 @@
                 start = whole[hi : hi + 1] if i < blocks - 1 else jnp.zeros((1, kw), F32)
             power = jnp.where(past, start - whole, jnp.where(inside, -block, -jnp.inf))
             mults[d, i] = jnp.exp(power)
-    each(seqs, 1, lambda d: total_copy(d).start())
+    if rounds > 1:
+        met(1)
 
     own_copy.wait()
     for copy in w_copies:
         copy.wait()
     acc[...] = dot(feat[h], w_s[h])
     gather.hand_on(1, 0)
+    for r in range(2, rounds):
+        met(r)
+    each(seqs, 1, lambda d: total_copy(d).start())
     for c in range(CHUNKS):
         gather.side(0, c).wait_recv()
     acc[...] += dot(feat[gather.sib], w_s[gather.sib])
@@ -383,7 +405,7 @@
         return pl.pallas_call(
             functools.partial(kernel, heads, seqs),
             out_shape=jax.ShapeDtypeStruct((rows, ow), BF16),
-            in_specs=[pl.BlockSpec(memory_space=pl.ANY)] * 7,
+            in_specs=[pl.BlockSpec(memory_space=pltpu.HBM)] * 7,
             out_specs=pl.BlockSpec(memory_space=pltpu.VMEM),
             scratch_shapes=[
                 pltpu.VMEM((heads, rows, width), BF16),
@@ -408,9 +430,10 @@
                 dma,
                 hop, hop, hop, hop, hop, hop, hop, hop,
                 dma((seqs,)), dma((seqs,)), dma((seqs,)), dma((seqs,)),
+                pltpu.SemaphoreType.REGULAR((max(1, (seqs - 1).bit_length()),)),
             ],
             compiler_params=pltpu.CompilerParams(
-                collective_id=0, has_side_effects=True, vmem_limit_bytes=40 * 1024 * 1024
+                collective_id=0, has_side_effects=True, vmem_limit_bytes=60 * 1024 * 1024
             ),
         )(features, w_query, w_key, w_value, w_gate, w_out, forget)
 

time: 32.9 us -> 26.1 us (0.79)
  the two profiles are of different devices: /device:TPU:15 before, /device:TPU:0 now
where the time goes in v2:
time: 26.1 us; the launch traced here: 26 us
  Pallas kernels  24.4 us (93%)
  local copies, waits for them, and re-layouts  1.57 us (6%)
    pallas_call x1, Pallas kernels, local(): pl.pallas_call(functools.partial(kernel, heads, seqs), out_shape=jax.Shap...  24.4 us
    unnamed x1, local copies, waits for them, and re-layouts  1.57 us

profile of v2, /device:TPU:0, one launch (start us, length us, event | category | flops | bytes accessed | tf_op | source)
XLA Modules:
  0.0 26.0 jit_solution(12290959632264127543)
XLA Ops:
  0.0 24.4 %shard_map.73 = bf16[256,256]{1,0:T(8,128)(2,1)} custom-call(bf16[256,256]{1,0:T(8,128)(2,1)} %feat_hbm.1, bf16[1024,128]{1,0:T(8,128)(2,1)} %wq_hbm.1, bf16[1024,128]{1,0:T(8,128)(2,1)} %wk_hbm.1, bf16[1024,256]{1,0:T(8,128)(2,1)} %wv_hbm.1, bf16[1024,256]{1,0:T(8,128)(2,1)} %wg_hbm.1, bf16[1024,1024]{1,0:T(8,128)(2,1)} %wo_hbm.1, ...), custom_call_target="tpu_custom_call" | custom-call | tf_op jit(solution)/shard_map/pallas_call | solution.py:405
  24.4 1.6 %copy.9 = bf16[256,256]{1,0:T(8,128)(2,1)} copy(bf16[256,256]{1,0:T(8,128)(2,1)} %shard_map.73) | data formatting | bytes 262144

commit v3 on v2

--- a/solution.py
+++ b/solution.py
@@ -137,6 +137,10 @@
         wo_copies.append(copy)
 
     def near(sem, d):
+        pl.semaphore_signal(
+            sem, inc=1, device_id={"seq": p + 1 - 2 * lax.rem(p, 2)}, device_id_type=MESH
+        )
+
         @pl.when(p >= d)
         def _():
             pl.semaphore_signal(sem, inc=1, device_id={"seq": p - d}, device_id_type=MESH)
@@ -146,7 +150,7 @@
             pl.semaphore_signal(sem, inc=1, device_id={"seq": p + d}, device_id_type=MESH)
 
     def near_count(d):
-        return jnp.where(p >= d, 1, 0) + jnp.where(p + d < seqs, 1, 0)
+        return 1 + jnp.where(p >= d, 1, 0) + jnp.where(p + d < seqs, 1, 0)
 
     barrier = pltpu.get_barrier_semaphore()
     sibling = h + 1 - 2 * lax.rem(h, 2)
@@ -155,16 +159,16 @@
         pl.semaphore_signal(
             barrier, inc=1, device_id={"head": lax.rem(h + j, heads)}, device_id_type=MESH
         )
-    near(barrier, 1)
-    pl.semaphore_wait(barrier, heads // 2 + near_count(1))
+    near(barrier, 2)
+    pl.semaphore_wait(barrier, heads // 2 + near_count(2))
 
     rounds = meet.shape[0]
-    near(meet.at[0], 1)
+    near(meet.at[0], 2)
 
     def met(r):
-        pl.semaphore_wait(meet.at[r], near_count(1 << r))
+        pl.semaphore_wait(meet.at[r], near_count(2 << r))
         if r + 1 < rounds:
-            near(meet.at[r + 1], 1 << (r + 1))
+            near(meet.at[r + 1], 2 << (r + 1))
 
     gather = HeadGather(heads, h, feat_hbm, feat, crows, fcs, fcr, fss, fsr)
     for c in range(CHUNKS):
@@ -430,10 +434,10 @@
                 dma,
                 hop, hop, hop, hop, hop, hop, hop, hop,
                 dma((seqs,)), dma((seqs,)), dma((seqs,)), dma((seqs,)),
-                pltpu.SemaphoreType.REGULAR((max(1, (seqs - 1).bit_length()),)),
+                pltpu.SemaphoreType.REGULAR((max(1, (seqs // 2 - 1).bit_length()),)),
             ],
             compiler_params=pltpu.CompilerParams(
-                collective_id=0, has_side_effects=True, vmem_limit_bytes=60 * 1024 * 1024
+                collective_id=0, has_side_effects=True, vmem_limit_bytes=56400000
             ),
         )(features, w_query, w_key, w_value, w_gate, w_out, forget)
 

time: 26.1 us -> 24.2 us (0.927)
  the two profiles are of different devices: /device:TPU:0 before, /device:TPU:15 now
where the time goes in v3:
time: 24.2 us; the launch traced here: 23.8 us
  Pallas kernels  23.1 us (95%)
  local copies, waits for them, and re-layouts  0.66 us (3%)
    pallas_call x1, Pallas kernels, local(): pl.pallas_call(functools.partial(kernel, heads, seqs), out_shape=jax.Shap...  23.1 us
    unnamed x1, local copies, waits for them, and re-layouts  0.66 us

profile of v3, /device:TPU:15, one launch (start us, length us, event | category | flops | bytes accessed | tf_op | source)
XLA Modules:
  0.0 23.8 jit_solution(7774636692518296060)
XLA Ops:
  0.0 23.1 %shard_map.73 = bf16[256,256]{1,0:T(8,128)(2,1)S(1)} custom-call(bf16[256,256]{1,0:T(8,128)(2,1)} %feat_hbm.1, bf16[1024,128]{1,0:T(8,128)(2,1)} %wq_hbm.1, bf16[1024,128]{1,0:T(8,128)(2,1)} %wk_hbm.1, bf16[1024,256]{1,0:T(8,128)(2,1)} %wv_hbm.1, bf16[1024,256]{1,0:T(8,128)(2,1)} %wg_hbm.1, bf16[1024,1024]{1,0:T(8,128)(2,1)} %wo_hbm.1, ...), custom_call_target="tpu_custom_call" | custom-call | tf_op jit(solution)/shard_map/pallas_call | solution.py:409
  23.1 0.7 %copy.9 = bf16[256,256]{1,0:T(8,128)(2,1)} copy(bf16[256,256]{1,0:T(8,128)(2,1)S(1)} %shard_map.73) | data formatting | bytes 262144

commit v4 on v3

--- a/solution.py
+++ b/solution.py
@@ -170,7 +170,8 @@
         if r + 1 < rounds:
             near(meet.at[r + 1], 2 << (r + 1))
 
-    gather = HeadGather(heads, h, feat_hbm, feat, crows, fcs, fcr, fss, fsr)
+    own_copy.wait()
+    gather = HeadGather(heads, h, feat.at[h], feat, crows, fcs, fcr, fss, fsr)
     for c in range(CHUNKS):
         gather.start(c)
 
@@ -224,7 +225,6 @@
     if rounds > 1:
         met(1)
 
-    own_copy.wait()
     for copy in w_copies:
         copy.wait()
     acc[...] = dot(feat[h], w_s[h])

time: 24.2 us -> 24.2 us (level)
  no operation moved by 1% of the time
where the time goes in v4:
time: 24.2 us; the launch traced here: 23.7 us
  Pallas kernels  23.1 us (95%)
  local copies, waits for them, and re-layouts  0.66 us (3%)
    pallas_call x1, Pallas kernels, local(): pl.pallas_call(functools.partial(kernel, heads, seqs), out_shape=jax.Shap...  23.1 us
    unnamed x1, local copies, waits for them, and re-layouts  0.66 us

profile of v4, /device:TPU:15, one launch (start us, length us, event | category | flops | bytes accessed | tf_op | source)
XLA Modules:
  0.0 23.7 jit_solution(8815616274660121210)
XLA Ops:
  0.0 23.1 %shard_map.73 = bf16[256,256]{1,0:T(8,128)(2,1)S(1)} custom-call(bf16[256,256]{1,0:T(8,128)(2,1)} %feat_hbm.1, bf16[1024,128]{1,0:T(8,128)(2,1)} %wq_hbm.1, bf16[1024,128]{1,0:T(8,128)(2,1)} %wk_hbm.1, bf16[1024,256]{1,0:T(8,128)(2,1)} %wv_hbm.1, bf16[1024,256]{1,0:T(8,128)(2,1)} %wg_hbm.1, bf16[1024,1024]{1,0:T(8,128)(2,1)} %wo_hbm.1, ...), custom_call_target="tpu_custom_call" | custom-call | tf_op jit(solution)/shard_map/pallas_call | solution.py:409
  23.1 0.7 %copy.9 = bf16[256,256]{1,0:T(8,128)(2,1)} copy(bf16[256,256]{1,0:T(8,128)(2,1)S(1)} %shard_map.73) | data formatting | bytes 262144
